TPU v7x, 32 devices: a whole 2x2x4 slice. The times are simulated.
32 devices in a mesh: pool: 2 (over x), pencil: 8 (over z, y), tgroup: 2 (over core).
Axes of the slice: x: 2, y: 2, z: 4, core: 2. Of those that a mesh axis runs over, the one named last changes fastest.
Arguments:
- dpsi: float32 [2, 4, 196608], P(None, 'pool', ('pencil', 'tgroup')), parts along dimension 1, may hold values from -6 to 6
- stick_cols: int32 [3072], replicated, may hold values from 0 to 16383, as said below
- pw_z: int32 [3072, 64], P('pencil'), may hold values from 0 to 127, as said below
- v_local: float32 [128, 16384], P('pencil'), may hold values from -6 to 6
- dv: float32 [128, 16384], P('pencil'), may hold values from -6 to 6
Outputs:
- h_dpsi: float32 [2, 4, 196608], P(None, 'pool', ('pencil', 'tgroup')), parts along dimension 1
There are 2 independent parts, one for each index of `pool`. A program takes and returns all parts, laid end to end along the dimension named above; an argument that names none is the same for every part. Nothing has to cross between parts.
Inputs may be any that keep to these rules, and one draw needn't show every extreme that they name: `stick_cols`: the 3072 values are distinct. `pw_z`: the 64 values of each row are distinct.
All inputs are finite; a program needn't handle non-finite values.
Results may differ from a plain program's by a relative error of at most 0.00007.
Values sent between devices are 32-bit elements; how exact they have to be, the bound alone decides.
No kernel may reach another device: no remote copies, remote signals or barrier semaphores. Data moves between devices by JAX's collectives and lax.ppermute only.
A program may use at most 128 MiB of HBM per device.

v0:
```python
import math

import jax
import jax.numpy as jnp
import numpy as np
from jax import lax
from jax.experimental import pallas as pl
from jax.experimental.pallas import tpu as pltpu
from jax.sharding import PartitionSpec as P


N = 128
LANES = 128
SUB = 8
GROUP = 8


def transform_matrix():
    phase = np.outer(np.arange(N), np.arange(N)) % N
    angle = phase.astype(np.float64) * (2.0 * math.pi / N)
    re = np.cos(angle) / math.sqrt(N)
    im = np.sin(angle) / math.sqrt(N)
    return np.block([[re, im], [-im, re]])


def const_split(table):
    bf = jnp.bfloat16
    t32 = np.asarray(table, np.float32)
    high = t32.astype(bf)
    low = (t32 - high.astype(np.float32)).astype(bf)
    return jnp.asarray(high), jnp.asarray(low)


def split(value):
    high = value.astype(jnp.bfloat16)
    low = (value - high.astype(jnp.float32)).astype(jnp.bfloat16)
    return high, low


def dot(a, b, dims):
    return lax.dot_general(a, b, (dims, ((), ())), preferred_element_type=jnp.float32)


def lane_gather(values, index):
    return jnp.take_along_axis(values, index, axis=1, mode="promise_in_bounds")


def stick_index_kernel(zpw):
    def body(pw_ref, inv_ref, twice_ref):
        sticks = inv_ref.shape[0]
        for at in range(0, sticks, LANES):
            w = min(LANES, sticks - at)
            pw = pw_ref[:, at : at + w]
            spread = lax.broadcasted_iota(jnp.int32, (N, w), 0)
            acc = jnp.full((N, w), -1, jnp.int32)
            for k in range(zpw):
                acc = jnp.where(pw[k : k + 1, :] == spread, k, acc)
            inv_ref[at : at + w, :] = acc.T
            twice_ref[at : at + w, :] = jnp.concatenate([pw, pw], axis=0).T

    return body


def up_kernel(blocks, rows, zpw):
    def body(own_ref, other_ref, inv_ref, high_ref, low_ref, *rest):
        outs = rest[:blocks]
        grid_ref, field_ref = rest[blocks:]
        me = lax.axis_index("pencil")
        first = lax.axis_index("tgroup") == 0
        pairs = inv_ref.shape[0] // 2
        half = pairs // 2

        def mine(ref, part):
            low = ref[part, pl.ds(0, half, stride=2), :]
            high = ref[part, pl.ds(1, half, stride=2), :]
            return jnp.where(first, low, high)

        for part in range(2):
            own = mine(own_ref, part)
            other = mine(other_ref, part)
            coeff = jnp.concatenate([jnp.where(first, own, other), jnp.where(first, other, own)], axis=0)
            for parity in range(2):
                index = inv_ref[pl.ds(parity, pairs, stride=2), :]
                value = lane_gather(coeff, jnp.maximum(index, 0) + parity * zpw)
                grid_ref[part, pl.ds(parity, pairs, stride=2), :] = jnp.where(index >= 0, value, 0.0)
        high, low = split(jnp.concatenate([grid_ref[0], grid_ref[1]], axis=1))
        left = jnp.concatenate([high_ref[...], low_ref[...], high_ref[...]], axis=1)
        right = jnp.concatenate([high, high, low], axis=1)
        field_ref[...] = dot(left, right, ((1,), (1,)))
        for d in range(blocks):
            outs[d][...] = field_ref[pl.ds(pl.multiple_of((me ^ d) * rows, SUB), rows), :]

    return body


def quarter_swap(value):
    top = jnp.concatenate([value[:N, :N], value[N:, :N]], axis=1)
    bottom = jnp.concatenate([value[:N, N:], value[N:, N:]], axis=1)
    return jnp.concatenate([top, bottom], axis=0)


def strides(planes):
    return planes + 1, 2 * planes + 1


def plane_kernel(blocks, per_block, sticks, planes):
    rows = 2 * planes
    fold = LANES // rows
    reach = N * N // fold
    reach_bits = reach.bit_length() - 1
    span = N // fold
    slots = per_block * LANES
    plane_rows = min(planes, SUB)
    along_stride, back_stride = strides(planes)

    def body(*refs):
        fields = refs[:blocks]
        smem_ref, cols_ref, v_ref, dv_ref, mh_ref, ml_ref, th_ref, tl_ref = refs[blocks : blocks + 8]
        outs = refs[blocks + 8 : 2 * blocks + 8]
        stick_ref, grid_ref, re_ref, im_ref, back_ref = refs[2 * blocks + 8 :]
        me = lax.axis_index("pencil")

        def right_apply(value, high_ref, low_ref):
            high, low = split(value)
            left = jnp.concatenate([high, low, high], axis=1)
            right = jnp.concatenate([high_ref[...], high_ref[...], low_ref[...]], axis=0)
            return dot(left, right, ((1,), (0,)))

        def left_apply(value, high_ref, low_ref):
            high, low = split(value)
            left = jnp.concatenate([high_ref[...], low_ref[...], high_ref[...]], axis=1)
            right = jnp.concatenate([high, high, low], axis=0)
            return dot(left, right, ((1,), (0,)))

        def each_stick(work):
            for q in range(blocks):
                for j in range(sticks):
                    work(q * slots + j, smem_ref[q * sticks + j])

        grid_ref[...] = jnp.zeros(grid_ref.shape, jnp.float32)
        for d in range(blocks):
            base = pl.multiple_of((me ^ d) * slots, LANES)
            for k in range(per_block):
                w = min(LANES, sticks - k * LANES)
                part = fields[d][:, k * LANES : k * LANES + w]
                sub = cols_ref[pl.ds((me ^ d) * per_block + k, 1), :w] >> reach_bits
                part = jnp.concatenate([jnp.where(sub == u, part, 0.0) for u in range(fold)], axis=0)
                stick_ref[pl.ds(base + k * LANES, w), :] = part.T

        def scatter(stick, place):
            value = stick_ref[pl.ds(stick, 1), :]
            pltpu.store(grid_ref.at[pl.ds(place, 1), :], value, mask=value != 0.0)

        each_stick(scatter)

        step = 2 * N // planes

        def along_load(i):
            pieces = []
            for t in range(step // fold):
                at = pl.multiple_of((i * (step // fold) + t) * N, N)
                tile = grid_ref[pl.ds(at, N), :].T
                for u in range(fold):
                    lo = u * rows
                    pieces.append(jnp.concatenate([tile[lo : lo + planes], tile[lo + planes : lo + rows]], axis=1))
            return jnp.concatenate(pieces, axis=0)

        def along_store(i, value):
            for x in range(step):
                at = ((x % fold) * span + i * (step // fold) + x // fold) * along_stride
                re_ref[pl.ds(at, planes), :] = value[x * planes : (x + 1) * planes, :N]
                im_ref[pl.ds(at, planes), :] = value[x * planes : (x + 1) * planes, N:]

        many = min(GROUP, N // step)

        def along(g, c):
            own = [g * many + j for j in range(many)]
            values = [along_load(i) for i in own]
            values = [right_apply(value, mh_ref, ml_ref) for value in values]
            for i, value in zip(own, values):
                along_store(i, value)
            return c

        lax.fori_loop(0, N // step // many, along, 0)

        def load_pair(pp):
            tops, bottoms = [], []
            for h in range(2):
                pick = pl.ds(pp * 2 + h, N, stride=along_stride)
                tops.append(re_ref[pick, :])
                bottoms.append(im_ref[pick, :])
            return jnp.concatenate([jnp.concatenate(tops, axis=1), jnp.concatenate(bottoms, axis=1)], axis=0)

        def weigh(pp, space):
            weights = []
            for h in range(2):
                plane = pp * 2 + h
                at = pl.ds((plane // plane_rows) * (plane_rows * N) + plane % plane_rows, N, stride=plane_rows)
                weights.append(v_ref[at, :] + dv_ref[at, :])
            weight = jnp.concatenate(weights, axis=1)
            return space * jnp.concatenate([weight, weight], axis=0)

        def store_pair(pp, last):
            for h in range(2):
                for part in range(2):
                    at = pl.ds(part * planes + pp * 2 + h, N, stride=back_stride)
                    back_ref[at, :] = last[h * N : (h + 1) * N, part * N : (part + 1) * N]

        group = min(GROUP, planes // 2)

        def pairs(i, c):
            own = [i * group + j for j in range(group)]
            values = [left_apply(load_pair(pp), th_ref, tl_ref) for pp in own]
            values = [weigh(pp, value) for pp, value in zip(own, values)]
            values = [left_apply(value, mh_ref, ml_ref) for value in values]
            values = [right_apply(quarter_swap(value), th_ref, tl_ref) for value in values]
            for pp, value in zip(own, values):
                store_pair(pp, value)
            return c

        lax.fori_loop(0, planes // 2 // group, pairs, 0)

        def turn(g, c):
            for j in range(4):
                i = g * 4 + j
                pieces = []
                for u in range(fold):
                    at = (u * span + i) * back_stride
                    pieces.append(back_ref[pl.ds(at, rows), :])
                grid_ref[pl.ds(pl.multiple_of(i * N, N), N), :] = jnp.concatenate(pieces, axis=0).T
            return c

        lax.fori_loop(0, span // 4, turn, 0)

        def fetch(stick, place):
            stick_ref[pl.ds(stick, 1), :] = grid_ref[pl.ds(place, 1), :]

        each_stick(fetch)

        for d in range(blocks):
            for k in range(per_block):
                w = min(LANES, sticks - k * LANES)
                at = (me ^ d) * per_block + k
                tile = stick_ref[pl.ds(pl.multiple_of(at * LANES, LANES), LANES), :].T
                sub = cols_ref[pl.ds(at, 1), :] >> reach_bits
                value = tile[:rows]
                for u in range(1, fold):
                    value = jnp.where(sub == u, tile[u * rows : (u + 1) * rows], value)
                outs[d][:, k * LANES : k * LANES + w] = value[:, :w]

    return body


def down_kernel(blocks, rows, zpw):
    def body(*refs):
        fields = refs[:blocks]
        pw_ref, high_ref, low_ref, own_ref, other_ref, field_ref, grid_ref = refs[blocks:]
        me = lax.axis_index("pencil")
        first = lax.axis_index("tgroup") == 0
        for d in range(blocks):
            field_ref[pl.ds(pl.multiple_of((me ^ d) * rows, SUB), rows), :] = fields[d][...]
        high, low = split(field_ref[...])
        left = jnp.concatenate([high, low, high], axis=0)
        right = jnp.concatenate([high_ref[...], high_ref[...], low_ref[...]], axis=0)
        grid = dot(left, right, ((0,), (0,)))
        pairs = grid.shape[0] // 2
        half = pairs // 2
        even = pl.ds(0, pairs, stride=2)
        odd = pl.ds(1, pairs, stride=2)
        lane = lax.broadcasted_iota(jnp.int32, (pairs, LANES), 1)
        index = jnp.where(lane < zpw, pw_ref[even, :], pw_ref[odd, :])
        for part in range(2):
            grid_ref[part] = grid[:, part * N : (part + 1) * N]
            a = lane_gather(grid_ref[part, even, :], index)
            b = lane_gather(grid_ref[part, odd, :], index)
            picked = jnp.where(lane < zpw, a, b)
            own_ref[part] = jnp.where(first, picked[:half], picked[half:])
            other_ref[part] = jnp.where(first, picked[half:], picked[:half])

    return body


def call(body, outs, scratch, args, smem=(), room=16, flops=1 << 30):
    vmem = pl.BlockSpec(memory_space=pltpu.VMEM)
    scalar = pl.BlockSpec(memory_space=pltpu.SMEM)
    many = isinstance(outs, (list, tuple))
    return pl.pallas_call(
        body,
        out_shape=outs,
        in_specs=[scalar if i in smem else vmem for i in range(len(args))],
        out_specs=[vmem] * len(outs) if many else vmem,
        scratch_shapes=scratch,
        compiler_params=pltpu.CompilerParams(vmem_limit_bytes=room << 20),
        cost_estimate=pl.CostEstimate(flops=flops, bytes_accessed=1 << 20, transcendentals=0),
    )(*args)


def local(dpsi, stick_cols, pw_z, v_local, dv):
    blocks = lax.axis_size("pencil")
    bands = dpsi.shape[1]
    sticks, zpw = pw_z.shape
    planes = v_local.shape[0]
    rows = 2 * planes
    pairs = sticks // 2
    half = pairs // 2
    per_block = -(-sticks // LANES)
    f32 = jnp.float32

    matrix = transform_matrix()
    mh, ml = const_split(matrix)
    th, tl = const_split(matrix.T)
    order = np.arange(2 * N).reshape(2, blocks, planes).transpose(1, 0, 2).reshape(-1)
    uh, ul = const_split(matrix.T[order])
    dh, dl = const_split(matrix.T[order])

    swap = [(0, 1), (1, 0)]
    own = dpsi.reshape(2, bands, half, LANES).transpose(0, 2, 1, 3).reshape(2, half * bands, LANES)
    other = lax.ppermute(own, "tgroup", swap)

    lookup = jax.ShapeDtypeStruct((sticks, N), jnp.int32)
    inv, twice = call(stick_index_kernel(zpw), (lookup, lookup), [], (pw_z.T,))
    width = min(LANES, sticks)
    cols = stick_cols.reshape(blocks * per_block, width)
    if width < LANES:
        cols = jnp.pad(cols, ((0, 0), (0, LANES - width)), constant_values=-1)
    block = jax.ShapeDtypeStruct((rows, sticks), f32)
    fields = call(
        up_kernel(blocks, rows, zpw),
        [block] * blocks,
        [pltpu.VMEM((2, sticks, N), f32), pltpu.VMEM((2 * N, sticks), f32)],
        (own, other, inv, uh, ul),
    )

    def exchange(parts):
        got = [parts[0]]
        for d in range(1, blocks):
            got.append(lax.ppermute(parts[d], "pencil", [(i, i ^ d) for i in range(blocks)]))
        return got

    plane_rows = min(planes, SUB)

    def by_column(values):
        return (
            values.reshape(planes // plane_rows, plane_rows, N, N)
            .transpose(0, 2, 1, 3)
            .reshape(planes * N, N)
        )

    fold = LANES // rows
    along_stride, back_stride = strides(planes)
    applied = call(
        plane_kernel(blocks, per_block, sticks, planes),
        [block] * blocks,
        [
            pltpu.VMEM((blocks * per_block * LANES, LANES), f32),
            pltpu.VMEM((N // fold * N, LANES), f32),
            pltpu.VMEM((N * along_stride, N), f32),
            pltpu.VMEM((N * along_stride, N), f32),
            pltpu.VMEM((N * back_stride, N), f32),
        ],
        (*exchange(fields), stick_cols & (N * N // fold - 1), cols, by_column(v_local), by_column(dv), mh, ml, th, tl),
        smem=(blocks,),
        room=24,
        flops=1 << 33,
    )
    side = jax.ShapeDtypeStruct((2, half, LANES), f32)
    mine, theirs = call(
        down_kernel(blocks, rows, zpw),
        [side, side],
        [pltpu.VMEM((2 * N, sticks), f32), pltpu.VMEM((2, sticks, N), f32)],
        (*exchange(applied), twice, dh, dl),
    )
    back = lax.ppermute(theirs, "tgroup", swap)
    mine = mine.reshape(2, 1, half * LANES)
    back = back.reshape(2, 1, half * LANES)
    band = lax.broadcasted_iota(jnp.int32, (2, bands, half * LANES), 1)
    return jnp.where(band == lax.axis_index("tgroup"), mine, back)


def solution(mesh):
    in_specs = (
        P(None, "pool", ("pencil", "tgroup")),
        P(),
        P("pencil", None),
        P("pencil", None),
        P("pencil", None),
    )
    out_specs = P(None, "pool", ("pencil", "tgroup"))

    return jax.shard_map(local, mesh=mesh, in_specs=in_specs, out_specs=out_specs, check_vma=False)
```

profile of v0, /device:TPU:0, one launch (start us, length us, event | category | flops | bytes accessed | tf_op | source)
XLA Modules:
  0.0 48.7 jit_solution(5731641010554110658)
XLA Ops:
  0.0 0.5 %collective-permute-start = (f32[2,192,128]{2,1,0:T(8,128)}, f32[2,192,128]{2,1,0:T(8,128)S(1)}, u32[]{:S(2)}, u32[]{:S(2)}) collective-permute-start(f32[2,192,128]{2,1,0:T(8,128)} %bitcast.29), channel_id=1, source_target_pairs={{0,1},{1,0},{2,3},{3,2},{4,5},{5,4},{6,7},{7,6},{8,9},{9,8},{10,11... | collective-permute-start | bytes 589832 | tf_op jit(solution)/shard_map/ppermute | solution.py:318
  0.5 0.9 %copy-done.4 = s32[384,64]{0,1:T(8,128)S(1)} copy-done((s32[384,64]{0,1:T(8,128)S(1)}, s32[384,64]{0,1:T(8,128)}, u32[]{:S(2)}) %copy-start.4) | copy-done | bytes 98328
  1.4 1.2 %shard_map.127 = (s32[384,128]{1,0:T(8,128)S(1)}, s32[384,128]{1,0:T(8,128)S(1)}) custom-call(s32[64,384]{1,0:T(8,128)S(1)} %bitcast.31), custom_call_target="tpu_custom_call" | custom-call | flops 1073741824 | bytes 1048576 | tf_op jit(solution)/shard_map/pallas_call | solution.py:287
  2.6 0.0 collective-permute-done.other_ref
  2.6 0.0 copy-start.1
  2.7 0.0 copy-start.2
  2.7 0.0 copy-start.7
  2.7 0.0 copy-start.8
  2.7 0.0 copy-start.9
  2.7 0.0 copy-start.10
  2.7 0.8 %shard_map.128 = (f32[32,384]{1,0:T(8,128)S(1)}, f32[32,384]{1,0:T(8,128)S(1)}, f32[32,384]{1,0:T(8,128)S(1)}, f32[32,384]{1,0:T(8,128)S(1)}, f32[32,384]{1,0:T(...) custom-call(f32[2,192,128]{2,1,0:T(8,128)S(1)} %bitcast.30, ...), custom_call_target="tpu_custom_call" | custom-call | flops 1073741824 | bytes 1048576 | tf_op jit(solution)/shard_map/pallas_call | solution.py:287
  3.5 0.0 copy-start
  3.5 2.6 %collective-permute-start.1 = (f32[32,384]{1,0:T(8,128)S(1)}, f32[32,384]{1,0:T(8,128)S(1)}, u32[]{:S(2)}, u32[]{:S(2)}) collective-permute-start(f32[32,384]{1,0:T(8,128)S(1)} %get-tuple-element.27), channel_id=1, source_target_pairs={{0,2},{2,0},{4,6},{6,4},{8,10},{10,8},{12,14},{14,12},{1,3},{3,1},... | collective-permute-start | bytes 147464 | tf_op jit(solution)/shard_map/ppermute | solution.py:337
  6.1 1.6 %collective-permute-start.2 = (f32[32,384]{1,0:T(8,128)S(1)}, f32[32,384]{1,0:T(8,128)S(1)}, u32[]{:S(2)}, u32[]{:S(2)}) collective-permute-start(f32[32,384]{1,0:T(8,128)S(1)} %get-tuple-element.28), channel_id=1, source_target_pairs={{0,4},{2,6},{4,0},{6,2},{8,12},{10,14},{12,8},{14,10},{1,5},{3,7},... | collective-permute-start | bytes 147464 | tf_op jit(solution)/shard_map/ppermute | solution.py:337
  7.7 0.0 collective-permute-start.3
  7.7 3.0 %collective-permute-start.4 = (f32[32,384]{1,0:T(8,128)S(1)}, f32[32,384]{1,0:T(8,128)S(1)}, u32[]{:S(2)}, u32[]{:S(2)}) collective-permute-start(f32[32,384]{1,0:T(8,128)S(1)} %get-tuple-element.30), channel_id=1, source_target_pairs={{0,8},{2,10},{4,12},{6,14},{8,0},{10,2},{12,4},{14,6},{1,9},{3,11}... | collective-permute-start | bytes 147464 | tf_op jit(solution)/shard_map/ppermute | solution.py:337
  10.7 1.3 %collective-permute-start.5 = (f32[32,384]{1,0:T(8,128)S(1)}, f32[32,384]{1,0:T(8,128)S(1)}, u32[]{:S(2)}, u32[]{:S(2)}) collective-permute-start(f32[32,384]{1,0:T(8,128)S(1)} %get-tuple-element.31), channel_id=1, source_target_pairs={{0,10},{2,8},{4,14},{6,12},{8,2},{10,0},{12,6},{14,4},{1,11},{3,9}... | collective-permute-start | bytes 147464 | tf_op jit(solution)/shard_map/ppermute | solution.py:337
  11.9 0.0 collective-permute-done.1.refs_1_
  11.9 3.6 %collective-permute-start.6 = (f32[32,384]{1,0:T(8,128)S(1)}, f32[32,384]{1,0:T(8,128)S(1)}, u32[]{:S(2)}, u32[]{:S(2)}) collective-permute-start(f32[32,384]{1,0:T(8,128)S(1)} %get-tuple-element.32), channel_id=1, source_target_pairs={{0,12},{2,14},{4,8},{6,10},{8,4},{10,6},{12,0},{14,2},{1,13},{3,15... | collective-permute-start | bytes 147464 | tf_op jit(solution)/shard_map/ppermute | solution.py:337
  15.6 0.0 collective-permute-done.2.refs_2_
  15.6 0.0 collective-permute-start.7
  15.6 0.0 collective-permute-done.3.refs_3_
  15.6 0.0 collective-permute-done.4.refs_4_
  15.6 3.0 %collective-permute-done.5.refs_5_ = f32[32,384]{1,0:T(8,128)S(1)} collective-permute-done((f32[32,384]{1,0:T(8,128)S(1)}, f32[32,384]{1,0:T(8,128)S(1)}, u32[]{:S(2)}, u32[]{:S(2)}) %collective-permute-start.5) | collective-permute-done | bytes 49184 | tf_op jit(solution)/shard_map/ppermute | solution.py:337
  18.6 0.0 collective-permute-done.6.refs_6_
  18.6 3.7 %collective-permute-done.7.refs_7_ = f32[32,384]{1,0:T(8,128)S(1)} collective-permute-done((f32[32,384]{1,0:T(8,128)S(1)}, f32[32,384]{1,0:T(8,128)S(1)}, u32[]{:S(2)}, u32[]{:S(2)}) %collective-permute-start.7) | collective-permute-done | bytes 49184 | tf_op jit(solution)/shard_map/ppermute | solution.py:337
  22.3 0.0 copy-done.2
  22.4 10.5 %shard_map.129 = (f32[32,384]{1,0:T(8,128)S(1)}, f32[32,384]{1,0:T(8,128)S(1)}, f32[32,384]{1,0:T(8,128)S(1)}, f32[32,384]{1,0:T(8,128)S(1)}, f32[32,384]{1,0:T(...) custom-call(f32[32,384]{1,0:T(8,128)S(1)} %get-tuple-element.26.refs_0_, ...), custom_call_target="tpu_custom_call" | custom-call | flops 8589934592 | bytes 1048576 | tf_op jit(solution)/shard_map/pallas_call | solution.py:287
  32.8 0.1 collective-permute-start.10
  32.9 1.2 %collective-permute-start.11 = (f32[32,384]{1,0:T(8,128)S(1)}, f32[32,384]{1,0:T(8,128)S(1)}, u32[]{:S(2)}, u32[]{:S(2)}) collective-permute-start(f32[32,384]{1,0:T(8,128)S(1)} %get-tuple-element.38), channel_id=1, source_target_pairs={{0,8},{2,10},{4,12},{6,14},{8,0},{10,2},{12,4},{14,6},{1,9},{3,11}... | collective-permute-start | bytes 147464 | tf_op jit(solution)/shard_map/ppermute | solution.py:337
  34.1 1.7 %collective-permute-start.12 = (f32[32,384]{1,0:T(8,128)S(1)}, f32[32,384]{1,0:T(8,128)S(1)}, u32[]{:S(2)}, u32[]{:S(2)}) collective-permute-start(f32[32,384]{1,0:T(8,128)S(1)} %get-tuple-element.39), channel_id=1, source_target_pairs={{0,10},{2,8},{4,14},{6,12},{8,2},{10,0},{12,6},{14,4},{1,11},{3,9}... | collective-permute-start | bytes 147464 | tf_op jit(solution)/shard_map/ppermute | solution.py:337
  35.8 3.2 %collective-permute-start.13 = (f32[32,384]{1,0:T(8,128)S(1)}, f32[32,384]{1,0:T(8,128)S(1)}, u32[]{:S(2)}, u32[]{:S(2)}) collective-permute-start(f32[32,384]{1,0:T(8,128)S(1)} %get-tuple-element.40), channel_id=1, source_target_pairs={{0,12},{2,14},{4,8},{6,10},{8,4},{10,6},{12,0},{14,2},{1,13},{3,15... | collective-permute-start | bytes 147464 | tf_op jit(solution)/shard_map/ppermute | solution.py:337
  39.0 1.6 %collective-permute-start.14 = (f32[32,384]{1,0:T(8,128)S(1)}, f32[32,384]{1,0:T(8,128)S(1)}, u32[]{:S(2)}, u32[]{:S(2)}) collective-permute-start(f32[32,384]{1,0:T(8,128)S(1)} %get-tuple-element.41), channel_id=1, source_target_pairs={{0,14},{2,12},{4,10},{6,8},{8,6},{10,4},{12,2},{14,0},{1,15},{3,13... | collective-permute-start | bytes 147464 | tf_op jit(solution)/shard_map/ppermute | solution.py:337
  40.6 0.0 collective-permute-done.10.refs_3_
  40.6 0.5 %collective-permute-start.8 = (f32[32,384]{1,0:T(8,128)S(1)}, f32[32,384]{1,0:T(8,128)S(1)}, u32[]{:S(2)}, u32[]{:S(2)}) collective-permute-start(f32[32,384]{1,0:T(8,128)S(1)} %get-tuple-element.35), channel_id=1, source_target_pairs={{0,2},{2,0},{4,6},{6,4},{8,10},{10,8},{12,14},{14,12},{1,3},{3,1},... | collective-permute-start | bytes 147464 | tf_op jit(solution)/shard_map/ppermute | solution.py:337
  41.1 0.0 collective-permute-done.11.refs_4_
  41.1 1.1 %collective-permute-start.9 = (f32[32,384]{1,0:T(8,128)S(1)}, f32[32,384]{1,0:T(8,128)S(1)}, u32[]{:S(2)}, u32[]{:S(2)}) collective-permute-start(f32[32,384]{1,0:T(8,128)S(1)} %get-tuple-element.36), channel_id=1, source_target_pairs={{0,4},{2,6},{4,0},{6,2},{8,12},{10,14},{12,8},{14,10},{1,5},{3,7},... | collective-permute-start | bytes 147464 | tf_op jit(solution)/shard_map/ppermute | solution.py:337
  42.3 0.0 collective-permute-done.12.refs_5_
  42.3 0.0 collective-permute-done.13.refs_6_
  42.3 3.6 %collective-permute-done.14.refs_7_ = f32[32,384]{1,0:T(8,128)S(1)} collective-permute-done((f32[32,384]{1,0:T(8,128)S(1)}, f32[32,384]{1,0:T(8,128)S(1)}, u32[]{:S(2)}, u32[]{:S(2)}) %collective-permute-start.14) | collective-permute-done | bytes 49184 | tf_op jit(solution)/shard_map/ppermute | solution.py:337
  45.8 0.0 collective-permute-done.8.refs_1_
  45.8 0.0 collective-permute-done.9.refs_2_
  45.8 0.6 %shard_map.130 = (f32[2,96,128]{2,1,0:T(8,128)S(1)}, f32[2,96,128]{2,1,0:T(8,128)S(1)}) custom-call(f32[32,384]{1,0:T(8,128)S(1)} %get-tuple-element.34.refs_0_, f32[32,384]{1,0:T(8,128)S(1)} %collective-permute-done.8.refs_1_, f32[32,384]{1,0:T(8,128)S(1)} %collective-permute-done.9.refs_2_, f32[32,384]{1,0:T(8,128)S(1)} %collective-permute-done.10.refs_3_, ...), custom_call_target="tpu_custom_call" | custom-call | flops 1073741824 | bytes 1048576 | tf_op jit(solution)/shard_map/pallas_call | solution.py:287
  46.4 0.1 collective-permute-start.15
  46.5 0.1 copy.20
  46.6 1.2 %collective-permute-done.15 = f32[2,96,128]{2,1,0:T(8,128)S(1)} collective-permute-done((f32[2,96,128]{2,1,0:T(8,128)S(1)}, f32[2,96,128]{2,1,0:T(8,128)S(1)}, u32[]{:S(2)}, u32[]{:S(2)}) %collective-permute-start.15) | collective-permute-done | bytes 98336 | tf_op jit(solution)/shard_map/ppermute | solution.py:373
  47.8 0.1 copy.19
  47.9 0.8 %broadcast_select_fusion = f32[2,2,12288]{2,1,0:T(2,128)} fusion(pred[2]{0:T(512)(128)(4,1)S(1)} %iota_compare_fusion, f32[2,12288]{1,0:T(2,128)S(1)} %bitcast.33, f32[2,12288]{1,0:T(2,128)S(1)} %bitcast.32), kind=kLoop, calls=%fused_computation | loop fusion | flops 49152 | bytes 393218 | tf_op jit(solution)/shard_map/jit(_where)/select_n | solution.py:377
  (15 shorter events, 0.0 us)
Async XLA Ops:
  0.0 2.6 %collective-permute-start = (f32[2,192,128]{2,1,0:T(8,128)}, f32[2,192,128]{2,1,0:T(8,128)S(1)}, u32[]{:S(2)}, u32[]{:S(2)}) collective-permute-start(f32[2,192,128]{2,1,0:T(8,128)} %bitcast.29), channel_id=1, source_target_pairs={{0,1},{1,0},{2,3},{3,2},{4,5},{5,4},{6,7},{7,6},{8,9},{9,8},{10,11... | collective-permute-start | bytes 589832 | tf_op jit(solution)/shard_map/ppermute | solution.py:318
  0.5 0.9 %copy-start.4 = (s32[384,64]{0,1:T(8,128)S(1)}, s32[384,64]{0,1:T(8,128)}, u32[]{:S(2)}) copy-start(s32[384,64]{0,1:T(8,128)} %param.15) | copy-start | bytes 294916
  1.4 1.2 %copy-start.3 = (f32[2,2,12288]{2,1,0:T(2,128)S(1)}, f32[2,2,12288]{2,1,0:T(2,128)}, u32[]{:S(2)}) copy-start(f32[2,2,12288]{2,1,0:T(2,128)} %param.13) | copy-start | bytes 589828
  1.4 1.2 %copy-start.5 = (bf16[256,256]{1,0:T(8,128)(2,1)S(1)}, bf16[256,256]{1,0:T(8,128)(2,1)}, u32[]{:S(2)}) copy-start(bf16[256,256]{1,0:T(8,128)(2,1)} %constant.22.clone.high_ref.refs_9_) | copy-start | bytes 393220
  1.4 1.2 %copy-start.6 = (bf16[256,256]{1,0:T(8,128)(2,1)S(1)}, bf16[256,256]{1,0:T(8,128)(2,1)}, u32[]{:S(2)}) copy-start(bf16[256,256]{1,0:T(8,128)(2,1)} %constant.23.clone.low_ref.refs_10_) | copy-start | bytes 393220
  2.6 19.7 %copy-start.1 = (f32[16,16384]{1,0:T(8,128)S(1)}, f32[16,16384]{1,0:T(8,128)}, u32[]{:S(2)}) copy-start(f32[16,16384]{1,0:T(8,128)} %param.16) | copy-start | bytes 3145732
  2.7 19.7 %copy-start.2 = (f32[16,16384]{1,0:T(8,128)S(1)}, f32[16,16384]{1,0:T(8,128)}, u32[]{:S(2)}) copy-start(f32[16,16384]{1,0:T(8,128)} %param.17) | copy-start | bytes 3145732
  2.7 19.7 %copy-start.7 = (bf16[256,256]{1,0:T(8,128)(2,1)S(1)}, bf16[256,256]{1,0:T(8,128)(2,1)}, u32[]{:S(2)}) copy-start(bf16[256,256]{1,0:T(8,128)(2,1)} %constant.18.clone.refs_12_) | copy-start | bytes 393220
  2.7 19.7 %copy-start.8 = (bf16[256,256]{1,0:T(8,128)(2,1)S(1)}, bf16[256,256]{1,0:T(8,128)(2,1)}, u32[]{:S(2)}) copy-start(bf16[256,256]{1,0:T(8,128)(2,1)} %constant.19.clone.refs_13_) | copy-start | bytes 393220
  2.7 19.7 %copy-start.9 = (bf16[256,256]{1,0:T(8,128)(2,1)S(1)}, bf16[256,256]{1,0:T(8,128)(2,1)}, u32[]{:S(2)}) copy-start(bf16[256,256]{1,0:T(8,128)(2,1)} %constant.20.clone.refs_14_) | copy-start | bytes 393220
  2.7 19.7 %copy-start.10 = (bf16[256,256]{1,0:T(8,128)(2,1)S(1)}, bf16[256,256]{1,0:T(8,128)(2,1)}, u32[]{:S(2)}) copy-start(bf16[256,256]{1,0:T(8,128)(2,1)} %constant.21.clone.refs_15_) | copy-start | bytes 393220
  3.5 12.1 %copy-start = (s32[3072]{0:T(1024)S(1)}, s32[3072]{0:T(1024)}, u32[]{:S(2)}) copy-start(s32[3072]{0:T(1024)} %param.14) | copy-start | bytes 36868
  3.5 8.4 %collective-permute-start.1 = (f32[32,384]{1,0:T(8,128)S(1)}, f32[32,384]{1,0:T(8,128)S(1)}, u32[]{:S(2)}, u32[]{:S(2)}) collective-permute-start(f32[32,384]{1,0:T(8,128)S(1)} %get-tuple-element.27), channel_id=1, source_target_pairs={{0,2},{2,0},{4,6},{6,4},{8,10},{10,8},{12,14},{14,12},{1,3},{3,1},... | collective-permute-start | bytes 147464 | tf_op jit(solution)/shard_map/ppermute | solution.py:337
  6.1 9.5 %collective-permute-start.2 = (f32[32,384]{1,0:T(8,128)S(1)}, f32[32,384]{1,0:T(8,128)S(1)}, u32[]{:S(2)}, u32[]{:S(2)}) collective-permute-start(f32[32,384]{1,0:T(8,128)S(1)} %get-tuple-element.28), channel_id=1, source_target_pairs={{0,4},{2,6},{4,0},{6,2},{8,12},{10,14},{12,8},{14,10},{1,5},{3,7},... | collective-permute-start | bytes 147464 | tf_op jit(solution)/shard_map/ppermute | solution.py:337
  7.7 7.9 %collective-permute-start.3 = (f32[32,384]{1,0:T(8,128)S(1)}, f32[32,384]{1,0:T(8,128)S(1)}, u32[]{:S(2)}, u32[]{:S(2)}) collective-permute-start(f32[32,384]{1,0:T(8,128)S(1)} %get-tuple-element.29), channel_id=1, source_target_pairs={{0,6},{2,4},{4,2},{6,0},{8,14},{10,12},{12,10},{14,8},{1,7},{3,5},... | collective-permute-start | bytes 147464 | tf_op jit(solution)/shard_map/ppermute | solution.py:337
  7.7 7.9 %collective-permute-start.4 = (f32[32,384]{1,0:T(8,128)S(1)}, f32[32,384]{1,0:T(8,128)S(1)}, u32[]{:S(2)}, u32[]{:S(2)}) collective-permute-start(f32[32,384]{1,0:T(8,128)S(1)} %get-tuple-element.30), channel_id=1, source_target_pairs={{0,8},{2,10},{4,12},{6,14},{8,0},{10,2},{12,4},{14,6},{1,9},{3,11}... | collective-permute-start | bytes 147464 | tf_op jit(solution)/shard_map/ppermute | solution.py:337
  10.7 8.0 %collective-permute-start.5 = (f32[32,384]{1,0:T(8,128)S(1)}, f32[32,384]{1,0:T(8,128)S(1)}, u32[]{:S(2)}, u32[]{:S(2)}) collective-permute-start(f32[32,384]{1,0:T(8,128)S(1)} %get-tuple-element.31), channel_id=1, source_target_pairs={{0,10},{2,8},{4,14},{6,12},{8,2},{10,0},{12,6},{14,4},{1,11},{3,9}... | collective-permute-start | bytes 147464 | tf_op jit(solution)/shard_map/ppermute | solution.py:337
  11.9 6.7 %collective-permute-start.6 = (f32[32,384]{1,0:T(8,128)S(1)}, f32[32,384]{1,0:T(8,128)S(1)}, u32[]{:S(2)}, u32[]{:S(2)}) collective-permute-start(f32[32,384]{1,0:T(8,128)S(1)} %get-tuple-element.32), channel_id=1, source_target_pairs={{0,12},{2,14},{4,8},{6,10},{8,4},{10,6},{12,0},{14,2},{1,13},{3,15... | collective-permute-start | bytes 147464 | tf_op jit(solution)/shard_map/ppermute | solution.py:337
  15.6 6.8 %collective-permute-start.7 = (f32[32,384]{1,0:T(8,128)S(1)}, f32[32,384]{1,0:T(8,128)S(1)}, u32[]{:S(2)}, u32[]{:S(2)}) collective-permute-start(f32[32,384]{1,0:T(8,128)S(1)} %get-tuple-element.33), channel_id=1, source_target_pairs={{0,14},{2,12},{4,10},{6,8},{8,6},{10,4},{12,2},{14,0},{1,15},{3,13... | collective-permute-start | bytes 147464 | tf_op jit(solution)/shard_map/ppermute | solution.py:337
  32.8 7.8 %collective-permute-start.10 = (f32[32,384]{1,0:T(8,128)S(1)}, f32[32,384]{1,0:T(8,128)S(1)}, u32[]{:S(2)}, u32[]{:S(2)}) collective-permute-start(f32[32,384]{1,0:T(8,128)S(1)} %get-tuple-element.37), channel_id=1, source_target_pairs={{0,6},{2,4},{4,2},{6,0},{8,14},{10,12},{12,10},{14,8},{1,7},{3,5},... | collective-permute-start | bytes 147464 | tf_op jit(solution)/shard_map/ppermute | solution.py:337
  32.9 8.2 %collective-permute-start.11 = (f32[32,384]{1,0:T(8,128)S(1)}, f32[32,384]{1,0:T(8,128)S(1)}, u32[]{:S(2)}, u32[]{:S(2)}) collective-permute-start(f32[32,384]{1,0:T(8,128)S(1)} %get-tuple-element.38), channel_id=1, source_target_pairs={{0,8},{2,10},{4,12},{6,14},{8,0},{10,2},{12,4},{14,6},{1,9},{3,11}... | collective-permute-start | bytes 147464 | tf_op jit(solution)/shard_map/ppermute | solution.py:337
  34.1 8.2 %collective-permute-start.12 = (f32[32,384]{1,0:T(8,128)S(1)}, f32[32,384]{1,0:T(8,128)S(1)}, u32[]{:S(2)}, u32[]{:S(2)}) collective-permute-start(f32[32,384]{1,0:T(8,128)S(1)} %get-tuple-element.39), channel_id=1, source_target_pairs={{0,10},{2,8},{4,14},{6,12},{8,2},{10,0},{12,6},{14,4},{1,11},{3,9}... | collective-permute-start | bytes 147464 | tf_op jit(solution)/shard_map/ppermute | solution.py:337
  35.8 6.4 %collective-permute-start.13 = (f32[32,384]{1,0:T(8,128)S(1)}, f32[32,384]{1,0:T(8,128)S(1)}, u32[]{:S(2)}, u32[]{:S(2)}) collective-permute-start(f32[32,384]{1,0:T(8,128)S(1)} %get-tuple-element.40), channel_id=1, source_target_pairs={{0,12},{2,14},{4,8},{6,10},{8,4},{10,6},{12,0},{14,2},{1,13},{3,15... | collective-permute-start | bytes 147464 | tf_op jit(solution)/shard_map/ppermute | solution.py:337
  39.0 6.8 %collective-permute-start.14 = (f32[32,384]{1,0:T(8,128)S(1)}, f32[32,384]{1,0:T(8,128)S(1)}, u32[]{:S(2)}, u32[]{:S(2)}) collective-permute-start(f32[32,384]{1,0:T(8,128)S(1)} %get-tuple-element.41), channel_id=1, source_target_pairs={{0,14},{2,12},{4,10},{6,8},{8,6},{10,4},{12,2},{14,0},{1,15},{3,13... | collective-permute-start | bytes 147464 | tf_op jit(solution)/shard_map/ppermute | solution.py:337
  40.6 5.2 %collective-permute-start.8 = (f32[32,384]{1,0:T(8,128)S(1)}, f32[32,384]{1,0:T(8,128)S(1)}, u32[]{:S(2)}, u32[]{:S(2)}) collective-permute-start(f32[32,384]{1,0:T(8,128)S(1)} %get-tuple-element.35), channel_id=1, source_target_pairs={{0,2},{2,0},{4,6},{6,4},{8,10},{10,8},{12,14},{14,12},{1,3},{3,1},... | collective-permute-start | bytes 147464 | tf_op jit(solution)/shard_map/ppermute | solution.py:337
  41.1 4.7 %collective-permute-start.9 = (f32[32,384]{1,0:T(8,128)S(1)}, f32[32,384]{1,0:T(8,128)S(1)}, u32[]{:S(2)}, u32[]{:S(2)}) collective-permute-start(f32[32,384]{1,0:T(8,128)S(1)} %get-tuple-element.36), channel_id=1, source_target_pairs={{0,4},{2,6},{4,0},{6,2},{8,12},{10,14},{12,8},{14,10},{1,5},{3,7},... | collective-permute-start | bytes 147464 | tf_op jit(solution)/shard_map/ppermute | solution.py:337
  46.4 1.4 %collective-permute-start.15 = (f32[2,96,128]{2,1,0:T(8,128)S(1)}, f32[2,96,128]{2,1,0:T(8,128)S(1)}, u32[]{:S(2)}, u32[]{:S(2)}) collective-permute-start(f32[2,96,128]{2,1,0:T(8,128)S(1)} %get-tuple-element.44), channel_id=1, source_target_pairs={{0,1},{1,0},{2,3},{3,2},{4,5},{5,4},{6,7},{7,6},{8,9},{9,8},{10,11... | collective-permute-start | bytes 294920 | tf_op jit(solution)/shard_map/ppermute | solution.py:373
where the time goes:
time: 48.8 us; the launch traced here: 48.7 us
  starting transfers between devices  22 us (45%)
  Pallas kernels  13 us (27%)
  waiting for transfers between devices  11.5 us (24%)
  local copies, waits for them, and re-layouts  1.11 us (2%)
  other arithmetic  0.85 us (2%)
    ppermute x14, starting transfers between devices, exchange(): lax.ppermute(parts[d], 'pencil', [(i, i ^ d) for i in range(blocks)])  21.4 us
    pallas_call x4, Pallas kernels, call(): pl.pallas_call(body, out_shape=outs, in_specs=[scalar if i in smem else v...  13 us
    ppermute x14, waiting for transfers between devices, exchange(): lax.ppermute(parts[d], 'pencil', [(i, i ^ d) for i in range(blocks)])  10.3 us
    ppermute x1, waiting for transfers between devices, local(): back = lax.ppermute(theirs, 'tgroup', swap)  1.19 us
    unnamed x24, local copies, waits for them, and re-layouts  1.11 us
  transfers between devices with their start and end apart: 16, of which 4 were waited for; matrix products, arithmetic and copies ran while one was open for 0% of the time, Pallas kernels for 2%

commit v1 on v0

--- a/solution.py
+++ b/solution.py
@@ -13,6 +13,8 @@
 LANES = 128
 SUB = 8
 GROUP = 8
+EXTRA = 1
+ORDER = (6, 4, 7, 5, 2, 3, 1)
 
 
 def transform_matrix():
@@ -51,21 +53,29 @@
         for at in range(0, sticks, LANES):
             w = min(LANES, sticks - at)
             pw = pw_ref[:, at : at + w]
-            spread = lax.broadcasted_iota(jnp.int32, (N, w), 0)
-            acc = jnp.full((N, w), -1, jnp.int32)
+            small = pw.astype(jnp.float32).astype(jnp.bfloat16)
+            spread = lax.broadcasted_iota(jnp.int32, (N, w), 0).astype(jnp.float32).astype(jnp.bfloat16)
+            acc = jnp.full((N, w), -1.0, jnp.bfloat16)
             for k in range(zpw):
-                acc = jnp.where(pw[k : k + 1, :] == spread, k, acc)
-            inv_ref[at : at + w, :] = acc.T
+                acc = jnp.where(small[k : k + 1, :] == spread, jnp.bfloat16(k), acc)
+            inv_ref[at : at + w, :] = acc.astype(jnp.float32).T.astype(jnp.int32)
             twice_ref[at : at + w, :] = jnp.concatenate([pw, pw], axis=0).T
 
     return body
 
 
-def up_kernel(blocks, rows, zpw):
-    def body(own_ref, other_ref, inv_ref, high_ref, low_ref, *rest):
+def up_kernel(blocks, rows, zpw, reach):
+    def body(own_ref, other_ref, inv_ref, high_ref, low_ref, all_ref, *rest):
         outs = rest[:blocks]
-        grid_ref, field_ref = rest[blocks:]
+        cols_ref, place_ref, grid_ref, field_ref = rest[blocks:]
         me = lax.axis_index("pencil")
+        per_block = cols_ref.shape[0] // blocks
+        for d in range(blocks):
+            for k in range(per_block):
+                row = all_ref[pl.ds((me ^ d) * per_block + k, 1), :]
+                at = d * per_block + k
+                cols_ref[at : at + 1, :] = row
+                place_ref[at : at + 1, :] = row & (reach - 1)
         first = lax.axis_index("tgroup") == 0
         pairs = inv_ref.shape[0] // 2
         half = pairs // 2
@@ -103,22 +113,78 @@
     return planes + 1, 2 * planes + 1
 
 
-def plane_kernel(blocks, per_block, sticks, planes):
+def place_sticks(ids, fields, smem_ref, cols_ref, stick_ref, grid_ref):
+    rows, sticks = fields[0].shape
+    fold = LANES // rows
+    reach_bits = (N * N // fold).bit_length() - 1
+    per_block = -(-sticks // LANES)
+    for n, d in enumerate(ids):
+        for k in range(per_block):
+            w = min(LANES, sticks - k * LANES)
+            part = fields[n][:, k * LANES : k * LANES + w]
+            sub = cols_ref[d * per_block + k : d * per_block + k + 1, :w] >> reach_bits
+            part = jnp.concatenate([jnp.where(sub == u, part, 0.0) for u in range(fold)], axis=0)
+            at = (n * per_block + k) * LANES
+            stick_ref[at : at + w, :] = part.T
+    for n, d in enumerate(ids):
+        for j in range(sticks):
+            at = n * per_block * LANES + j
+            value = stick_ref[at : at + 1, :]
+            pltpu.store(grid_ref.at[pl.ds(smem_ref[d * sticks + j], 1), :], value, mask=value != 0.0)
+
+
+def take_sticks(ids, outs, smem_ref, cols_ref, stick_ref, grid_ref):
+    rows, sticks = outs[0].shape
+    fold = LANES // rows
+    reach_bits = (N * N // fold).bit_length() - 1
+    per_block = -(-sticks // LANES)
+    for n, d in enumerate(ids):
+        for j in range(sticks):
+            at = n * per_block * LANES + j
+            stick_ref[at : at + 1, :] = grid_ref[pl.ds(smem_ref[d * sticks + j], 1), :]
+    for n, d in enumerate(ids):
+        for k in range(per_block):
+            w = min(LANES, sticks - k * LANES)
+            at = (n * per_block + k) * LANES
+            tile = stick_ref[at : at + LANES, :].T
+            sub = cols_ref[d * per_block + k : d * per_block + k + 1, :] >> reach_bits
+            value = tile[:rows]
+            for u in range(1, fold):
+                value = jnp.where(sub == u, tile[u * rows : (u + 1) * rows], value)
+            outs[n][:, k * LANES : k * LANES + w] = value[:, :w]
+
+
+def early_kernel(ids):
+    def body(*refs):
+        fields = refs[: len(ids)]
+        smem_ref, cols_ref, grid_ref, stick_ref = refs[len(ids) :]
+        grid_ref[...] = jnp.zeros(grid_ref.shape, jnp.float32)
+        place_sticks(ids, fields, smem_ref, cols_ref, stick_ref, grid_ref)
+
+    return body
+
+
+def late_kernel(ids):
+    def body(grid_ref, smem_ref, cols_ref, *rest):
+        take_sticks(ids, rest[:-1], smem_ref, cols_ref, rest[-1], grid_ref)
+
+    return body
+
+
+def plane_kernel(ids_in, ids_out, planes):
     rows = 2 * planes
     fold = LANES // rows
-    reach = N * N // fold
-    reach_bits = reach.bit_length() - 1
     span = N // fold
-    slots = per_block * LANES
     plane_rows = min(planes, SUB)
     along_stride, back_stride = strides(planes)
+    count_in, count_out = len(ids_in), len(ids_out)
 
     def body(*refs):
-        fields = refs[:blocks]
-        smem_ref, cols_ref, v_ref, dv_ref, mh_ref, ml_ref, th_ref, tl_ref = refs[blocks : blocks + 8]
-        outs = refs[blocks + 8 : 2 * blocks + 8]
-        stick_ref, grid_ref, re_ref, im_ref, back_ref = refs[2 * blocks + 8 :]
-        me = lax.axis_index("pencil")
+        fields = refs[:count_in]
+        _, smem_ref, cols_ref, v_ref, dv_ref, mh_ref, ml_ref, th_ref, tl_ref = refs[count_in : count_in + 9]
+        grid_ref = refs[count_in + 9]
+        outs = refs[count_in + 10 : count_in + 10 + count_out]
+        stick_ref, re_ref, im_ref, back_ref = refs[count_in + 10 + count_out :]
 
         def right_apply(value, high_ref, low_ref):
             high, low = split(value)
@@ -132,26 +198,7 @@
             right = jnp.concatenate([high, high, low], axis=0)
             return dot(left, right, ((1,), (0,)))
 
-        def each_stick(work):
-            for q in range(blocks):
-                for j in range(sticks):
-                    work(q * slots + j, smem_ref[q * sticks + j])
-
-        grid_ref[...] = jnp.zeros(grid_ref.shape, jnp.float32)
-        for d in range(blocks):
-            base = pl.multiple_of((me ^ d) * slots, LANES)
-            for k in range(per_block):
-                w = min(LANES, sticks - k * LANES)
-                part = fields[d][:, k * LANES : k * LANES + w]
-                sub = cols_ref[pl.ds((me ^ d) * per_block + k, 1), :w] >> reach_bits
-                part = jnp.concatenate([jnp.where(sub == u, part, 0.0) for u in range(fold)], axis=0)
-                stick_ref[pl.ds(base + k * LANES, w), :] = part.T
-
-        def scatter(stick, place):
-            value = stick_ref[pl.ds(stick, 1), :]
-            pltpu.store(grid_ref.at[pl.ds(place, 1), :], value, mask=value != 0.0)
-
-        each_stick(scatter)
+        place_sticks(ids_in, fields, smem_ref, cols_ref, stick_ref, grid_ref)
 
         step = 2 * N // planes
 
@@ -232,21 +279,7 @@
 
         lax.fori_loop(0, span // 4, turn, 0)
 
-        def fetch(stick, place):
-            stick_ref[pl.ds(stick, 1), :] = grid_ref[pl.ds(place, 1), :]
-
-        each_stick(fetch)
-
-        for d in range(blocks):
-            for k in range(per_block):
-                w = min(LANES, sticks - k * LANES)
-                at = (me ^ d) * per_block + k
-                tile = stick_ref[pl.ds(pl.multiple_of(at * LANES, LANES), LANES), :].T
-                sub = cols_ref[pl.ds(at, 1), :] >> reach_bits
-                value = tile[:rows]
-                for u in range(1, fold):
-                    value = jnp.where(sub == u, tile[u * rows : (u + 1) * rows], value)
-                outs[d][:, k * LANES : k * LANES + w] = value[:, :w]
+        take_sticks(ids_out, outs, smem_ref, cols_ref, stick_ref, grid_ref)
 
     return body
 
@@ -280,7 +313,7 @@
     return body
 
 
-def call(body, outs, scratch, args, smem=(), room=16, flops=1 << 30):
+def call(body, outs, scratch, args, smem=(), room=16, flops=1 << 30, alias=None):
     vmem = pl.BlockSpec(memory_space=pltpu.VMEM)
     scalar = pl.BlockSpec(memory_space=pltpu.SMEM)
     many = isinstance(outs, (list, tuple))
@@ -290,6 +323,7 @@
         in_specs=[scalar if i in smem else vmem for i in range(len(args))],
         out_specs=[vmem] * len(outs) if many else vmem,
         scratch_shapes=scratch,
+        input_output_aliases=alias or {},
         compiler_params=pltpu.CompilerParams(vmem_limit_bytes=room << 20),
         cost_estimate=pl.CostEstimate(flops=flops, bytes_accessed=1 << 20, transcendentals=0),
     )(*args)
@@ -317,25 +351,33 @@
     own = dpsi.reshape(2, bands, half, LANES).transpose(0, 2, 1, 3).reshape(2, half * bands, LANES)
     other = lax.ppermute(own, "tgroup", swap)
 
+    width = min(LANES, sticks)
+    columns = stick_cols.reshape(blocks * per_block, width)
+    if width < LANES:
+        columns = jnp.pad(columns, ((0, 0), (0, LANES - width)))
     lookup = jax.ShapeDtypeStruct((sticks, N), jnp.int32)
     inv, twice = call(stick_index_kernel(zpw), (lookup, lookup), [], (pw_z.T,))
-    width = min(LANES, sticks)
-    cols = stick_cols.reshape(blocks * per_block, width)
-    if width < LANES:
-        cols = jnp.pad(cols, ((0, 0), (0, LANES - width)), constant_values=-1)
+
     block = jax.ShapeDtypeStruct((rows, sticks), f32)
-    fields = call(
-        up_kernel(blocks, rows, zpw),
-        [block] * blocks,
+    near = jax.ShapeDtypeStruct(columns.shape, jnp.int32)
+    *fields, cols, places = call(
+        up_kernel(blocks, rows, zpw, N * N // (LANES // rows)),
+        [block] * blocks + [near, near],
         [pltpu.VMEM((2, sticks, N), f32), pltpu.VMEM((2 * N, sticks), f32)],
-        (own, other, inv, uh, ul),
+        (own, other, inv, uh, ul, columns),
     )
-
-    def exchange(parts):
-        got = [parts[0]]
-        for d in range(1, blocks):
-            got.append(lax.ppermute(parts[d], "pencil", [(i, i ^ d) for i in range(blocks)]))
-        return got
+    places = places[:, :width].reshape(-1)
+
+    order = issue_order(blocks)
+    early = [0] + order[: blocks // 2 - 1] + order[blocks // 2 : blocks // 2 + EXTRA]
+    rest = [d for d in order if d not in early]
+    ahead = order
+    behind = [0]
+
+    def send(part, d):
+        if d == 0:
+            return part
+        return lax.ppermute(part, "pencil", [(i, i ^ d) for i in range(blocks)])
 
     plane_rows = min(planes, SUB)
 
@@ -348,33 +390,54 @@
 
     fold = LANES // rows
     along_stride, back_stride = strides(planes)
-    applied = call(
-        plane_kernel(blocks, per_block, sticks, planes),
-        [block] * blocks,
+    reach = jax.ShapeDtypeStruct((N // fold * N, LANES), f32)
+
+    def room_for(ids):
+        return pltpu.VMEM((len(ids) * per_block * LANES, LANES), f32)
+
+    got = {d: send(fields[d], d) for d in range(blocks)}
+    grid = call(
+        early_kernel(early),
+        reach,
+        [room_for(early)],
+        (*[got[d] for d in early], places, cols),
+        smem=(len(early),),
+    )
+    count = len(rest)
+    grid, *first_out = call(
+        plane_kernel(rest, ahead, planes),
+        [reach] + [block] * len(ahead),
         [
-            pltpu.VMEM((blocks * per_block * LANES, LANES), f32),
-            pltpu.VMEM((N // fold * N, LANES), f32),
+            room_for(max(rest, ahead, key=len)),
             pltpu.VMEM((N * along_stride, N), f32),
             pltpu.VMEM((N * along_stride, N), f32),
             pltpu.VMEM((N * back_stride, N), f32),
         ],
-        (*exchange(fields), stick_cols & (N * N // fold - 1), cols, by_column(v_local), by_column(dv), mh, ml, th, tl),
-        smem=(blocks,),
+        (*[got[d] for d in rest], grid, places, cols, by_column(v_local), by_column(dv), mh, ml, th, tl),
+        smem=(count + 1,),
         room=24,
         flops=1 << 33,
+        alias={count: 0},
     )
+    last_out = call(late_kernel(behind), [block] * len(behind), [room_for(behind)], (grid, places, cols), smem=(1,))
+    applied = dict(zip(ahead + behind, list(first_out) + list(last_out)))
+    back = {d: send(applied[d], d) for d in range(blocks)}
     side = jax.ShapeDtypeStruct((2, half, LANES), f32)
     mine, theirs = call(
         down_kernel(blocks, rows, zpw),
         [side, side],
         [pltpu.VMEM((2 * N, sticks), f32), pltpu.VMEM((2, sticks, N), f32)],
-        (*exchange(applied), twice, dh, dl),
+        (*[back[d] for d in range(blocks)], twice, dh, dl),
     )
-    back = lax.ppermute(theirs, "tgroup", swap)
+    theirs = lax.ppermute(theirs, "tgroup", swap)
     mine = mine.reshape(2, 1, half * LANES)
-    back = back.reshape(2, 1, half * LANES)
+    back = theirs.reshape(2, 1, half * LANES)
     band = lax.broadcasted_iota(jnp.int32, (2, bands, half * LANES), 1)
     return jnp.where(band == lax.axis_index("tgroup"), mine, back)
+
+
+def issue_order(count):
+    return list(ORDER) if len(ORDER) == count - 1 else list(range(count - 1, 0, -1))
 
 
 def solution(mesh):

time: 48.8 us -> 45.7 us (0.936)
  waiting for transfers between devices: 11.5 us -> 5.46 us
  starting transfers between devices: 22 us -> 23.6 us
  Pallas kernels: 13 us -> 13.9 us
    ppermute x15, waiting for transfers between devices: 11.5 us -> 5.45 us  [the longest x14 4.26 us: send(): return lax.ppermute(part, 'pencil', [(i, i ^ d) for i in range(blocks)])]
    ppermute x15, starting transfers between devices: 21.5 us -> 23.1 us  [the longest x14 23 us: send(): return lax.ppermute(part, 'pencil', [(i, i ^ d) for i in range(blocks)])]
    pallas_call x4 -> x6, Pallas kernels: 13 us -> 13.9 us  [call(): pl.pallas_call(body, out_shape=outs, in_specs=[scalar if i in smem else v...]
  transfers between devices with their start and end apart: 16 -> 16, of which waited for: 4 -> 5; matrix products, arithmetic and copies ran while one was open for 0% -> 0% of each run, Pallas kernels for 2% -> 8%
where the time goes in v1:
time: 45.7 us; the launch traced here: 45.5 us
  starting transfers between devices  23.6 us (52%)
  Pallas kernels  13.9 us (30%)
  waiting for transfers between devices  5.46 us (12%)
  local copies, waits for them, and re-layouts  1.5 us (3%)
  other arithmetic  0.85 us (2%)
    ppermute x14, starting transfers between devices, send(): return lax.ppermute(part, 'pencil', [(i, i ^ d) for i in range(blocks)])  23 us
    pallas_call x6, Pallas kernels, call(): pl.pallas_call(body, out_shape=outs, in_specs=[scalar if i in smem else v...  13.9 us
    ppermute x14, waiting for transfers between devices, send(): return lax.ppermute(part, 'pencil', [(i, i ^ d) for i in range(blocks)])  4.26 us
    unnamed x24, local copies, waits for them, and re-layouts  1.5 us
    ppermute x1, waiting for transfers between devices, local(): theirs = lax.ppermute(theirs, 'tgroup', swap)  1.19 us
  transfers between devices with their start and end apart: 16, of which 5 were waited for; matrix products, arithmetic and copies ran while one was open for 0% of the time, Pallas kernels for 8%

profile of v1, /device:TPU:0, one launch (start us, length us, event | category | flops | bytes accessed | tf_op | source)
XLA Modules:
  0.0 45.5 jit_solution(6019680704280321365)
XLA Ops:
  0.0 0.5 %collective-permute-start = (f32[2,192,128]{2,1,0:T(8,128)}, f32[2,192,128]{2,1,0:T(8,128)S(1)}, u32[]{:S(2)}, u32[]{:S(2)}) collective-permute-start(f32[2,192,128]{2,1,0:T(8,128)} %bitcast.29), channel_id=1, source_target_pairs={{0,1},{1,0},{2,3},{3,2},{4,5},{5,4},{6,7},{7,6},{8,9},{9,8},{10,11... | collective-permute-start | bytes 589832 | tf_op jit(solution)/shard_map/ppermute | solution.py:352
  0.5 0.9 %copy-done.3 = s32[384,64]{0,1:T(8,128)S(1)} copy-done((s32[384,64]{0,1:T(8,128)S(1)}, s32[384,64]{0,1:T(8,128)}, u32[]{:S(2)}) %copy-start.3) | copy-done | bytes 98328
  1.4 0.6 %shard_map.127 = (s32[384,128]{1,0:T(8,128)S(1)}, s32[384,128]{1,0:T(8,128)S(1)}) custom-call(s32[64,384]{1,0:T(8,128)S(1)} %bitcast.31), custom_call_target="tpu_custom_call" | custom-call | flops 1073741824 | bytes 1048576 | tf_op jit(solution)/shard_map/pallas_call | solution.py:320
  2.0 0.0 collective-permute-done.other_ref
  2.0 0.1 copy-done.4
  2.1 0.2 copy-done.5
  2.3 0.1 copy-done.6
  2.4 0.8 %shard_map.128 = (f32[32,384]{1,0:T(8,128)S(1)}, f32[32,384]{1,0:T(8,128)S(1)}, f32[32,384]{1,0:T(8,128)S(1)}, f32[32,384]{1,0:T(8,128)S(1)}, f32[32,384]{1,0:T(...) custom-call(f32[2,192,128]{2,1,0:T(8,128)S(1)} %bitcast.30, ...), custom_call_target="tpu_custom_call" | custom-call | flops 1073741824 | bytes 1048576 | tf_op jit(solution)/shard_map/pallas_call | solution.py:320
  3.2 0.0 copy-start
  3.2 0.0 copy-start.1
  3.2 0.0 copy-start.7
  3.2 0.0 copy-start.8
  3.2 0.0 copy-start.9
  3.2 0.0 copy-start.10
  3.2 4.7 %collective-permute-start.4 = (f32[32,384]{1,0:T(8,128)S(1)}, f32[32,384]{1,0:T(8,128)S(1)}, u32[]{:S(2)}, u32[]{:S(2)}) collective-permute-start(f32[32,384]{1,0:T(8,128)S(1)} %get-tuple-element.32), channel_id=1, source_target_pairs={{0,12},{2,14},{4,8},{6,10},{8,4},{10,6},{12,0},{14,2},{1,13},{3,15... | collective-permute-start | bytes 147464 | tf_op jit(solution)/shard_map/ppermute | solution.py:380
  7.9 2.9 %collective-permute-start.6 = (f32[32,384]{1,0:T(8,128)S(1)}, f32[32,384]{1,0:T(8,128)S(1)}, u32[]{:S(2)}, u32[]{:S(2)}) collective-permute-start(f32[32,384]{1,0:T(8,128)S(1)} %get-tuple-element.34), channel_id=1, source_target_pairs={{0,14},{2,12},{4,10},{6,8},{8,6},{10,4},{12,2},{14,0},{1,15},{3,13... | collective-permute-start | bytes 147464 | tf_op jit(solution)/shard_map/ppermute | solution.py:380
  10.8 1.6 %collective-permute-start.7 = (f32[32,384]{1,0:T(8,128)S(1)}, f32[32,384]{1,0:T(8,128)S(1)}, u32[]{:S(2)}, u32[]{:S(2)}) collective-permute-start(f32[32,384]{1,0:T(8,128)S(1)} %get-tuple-element.35), channel_id=1, source_target_pairs={{0,4},{2,6},{4,0},{6,2},{8,12},{10,14},{12,8},{14,10},{1,5},{3,7},... | collective-permute-start | bytes 147464 | tf_op jit(solution)/shard_map/ppermute | solution.py:380
  12.4 0.8 %collective-permute-start.1 = (f32[32,384]{1,0:T(8,128)S(1)}, f32[32,384]{1,0:T(8,128)S(1)}, u32[]{:S(2)}, u32[]{:S(2)}) collective-permute-start(f32[32,384]{1,0:T(8,128)S(1)} %get-tuple-element.28), channel_id=1, source_target_pairs={{0,10},{2,8},{4,14},{6,12},{8,2},{10,0},{12,6},{14,4},{1,11},{3,9}... | collective-permute-start | bytes 147464 | tf_op jit(solution)/shard_map/ppermute | solution.py:380
  13.2 0.0 collective-permute-done.4.refs_1_
  13.2 1.0 %collective-permute-start.2 = (f32[32,384]{1,0:T(8,128)S(1)}, f32[32,384]{1,0:T(8,128)S(1)}, u32[]{:S(2)}, u32[]{:S(2)}) collective-permute-start(f32[32,384]{1,0:T(8,128)S(1)} %get-tuple-element.29), channel_id=1, source_target_pairs={{0,6},{2,4},{4,2},{6,0},{8,14},{10,12},{12,10},{14,8},{1,7},{3,5},... | collective-permute-start | bytes 147464 | tf_op jit(solution)/shard_map/ppermute | solution.py:380
  14.2 0.0 collective-permute-done.5.refs_2_
  14.2 1.8 %collective-permute-start.3 = (f32[32,384]{1,0:T(8,128)S(1)}, f32[32,384]{1,0:T(8,128)S(1)}, u32[]{:S(2)}, u32[]{:S(2)}) collective-permute-start(f32[32,384]{1,0:T(8,128)S(1)} %get-tuple-element.30), channel_id=1, source_target_pairs={{0,2},{2,0},{4,6},{6,4},{8,10},{10,8},{12,14},{14,12},{1,3},{3,1},... | collective-permute-start | bytes 147464 | tf_op jit(solution)/shard_map/ppermute | solution.py:380
  16.0 0.0 collective-permute-done.7.refs_4_
  16.0 2.0 %shard_map.129.refs_3_ = f32[4096,128]{1,0:T(8,128)S(1)} custom-call(f32[32,384]{1,0:T(8,128)S(1)} %get-tuple-element.31.refs_0_, f32[32,384]{1,0:T(8,128)S(1)} %collective-permute-done.4.refs_1_, f32[32,384]{1,0:T(8,128)S(1)} %collective-permute-done.5.refs_2_, f32[32,384]{1,0:T(8,128)S(1)} %collective-permute-done.6.refs_3_, ...), custom_call_target="tpu_custom_call" | custom-call | flops 1073741824 | bytes 1048576 | tf_op jit(solution)/shard_map/pallas_call | solution.py:320
  18.0 0.8 %collective-permute-done.1.refs_0_ = f32[32,384]{1,0:T(8,128)S(1)} collective-permute-done((f32[32,384]{1,0:T(8,128)S(1)}, f32[32,384]{1,0:T(8,128)S(1)}, u32[]{:S(2)}, u32[]{:S(2)}) %collective-permute-start.1) | collective-permute-done | bytes 49184 | tf_op jit(solution)/shard_map/ppermute | solution.py:380
  18.8 0.0 collective-permute-done.2.refs_1_
  18.8 0.4 collective-permute-done.3.refs_2_
  19.3 9.0 %shard_map.130 = (f32[4096,128]{1,0:T(8,128)S(1)}, f32[32,384]{1,0:T(8,128)S(1)}, f32[32,384]{1,0:T(8,128)S(1)}, f32[32,384]{1,0:T(8,128)S(1)}, f32[32,384]{1,0:...) custom-call(f32[32,384]{1,0:T(8,128)S(1)} %collective-permute-done.1, ...), custom_call_target="tpu_custom_call", output_to_operand_aliasing={{0}: (3, {})} | custom-call | flops 8589934592 | bytes 1048576 | tf_op jit(solution)/shard_map/pallas_call | solution.py:320
  28.3 1.0 %collective-permute-start.10 = (f32[32,384]{1,0:T(8,128)S(1)}, f32[32,384]{1,0:T(8,128)S(1)}, u32[]{:S(2)}, u32[]{:S(2)}) collective-permute-start(f32[32,384]{1,0:T(8,128)S(1)} %get-tuple-element.41), channel_id=1, source_target_pairs={{0,6},{2,4},{4,2},{6,0},{8,14},{10,12},{12,10},{14,8},{1,7},{3,5},... | collective-permute-start | bytes 147464 | tf_op jit(solution)/shard_map/ppermute | solution.py:380
  29.4 2.0 %collective-permute-start.11 = (f32[32,384]{1,0:T(8,128)S(1)}, f32[32,384]{1,0:T(8,128)S(1)}, u32[]{:S(2)}, u32[]{:S(2)}) collective-permute-start(f32[32,384]{1,0:T(8,128)S(1)} %get-tuple-element.42), channel_id=1, source_target_pairs={{0,8},{2,10},{4,12},{6,14},{8,0},{10,2},{12,4},{14,6},{1,9},{3,11}... | collective-permute-start | bytes 147464 | tf_op jit(solution)/shard_map/ppermute | solution.py:380
  31.4 1.9 %collective-permute-start.12 = (f32[32,384]{1,0:T(8,128)S(1)}, f32[32,384]{1,0:T(8,128)S(1)}, u32[]{:S(2)}, u32[]{:S(2)}) collective-permute-start(f32[32,384]{1,0:T(8,128)S(1)} %get-tuple-element.43), channel_id=1, source_target_pairs={{0,10},{2,8},{4,14},{6,12},{8,2},{10,0},{12,6},{14,4},{1,11},{3,9}... | collective-permute-start | bytes 147464 | tf_op jit(solution)/shard_map/ppermute | solution.py:380
  33.2 1.9 %collective-permute-start.13 = (f32[32,384]{1,0:T(8,128)S(1)}, f32[32,384]{1,0:T(8,128)S(1)}, u32[]{:S(2)}, u32[]{:S(2)}) collective-permute-start(f32[32,384]{1,0:T(8,128)S(1)} %get-tuple-element.44), channel_id=1, source_target_pairs={{0,12},{2,14},{4,8},{6,10},{8,4},{10,6},{12,0},{14,2},{1,13},{3,15... | collective-permute-start | bytes 147464 | tf_op jit(solution)/shard_map/ppermute | solution.py:380
  35.2 1.8 %collective-permute-start.14 = (f32[32,384]{1,0:T(8,128)S(1)}, f32[32,384]{1,0:T(8,128)S(1)}, u32[]{:S(2)}, u32[]{:S(2)}) collective-permute-start(f32[32,384]{1,0:T(8,128)S(1)} %get-tuple-element.45), channel_id=1, source_target_pairs={{0,14},{2,12},{4,10},{6,8},{8,6},{10,4},{12,2},{14,0},{1,15},{3,13... | collective-permute-start | bytes 147464 | tf_op jit(solution)/shard_map/ppermute | solution.py:380
  37.0 0.0 collective-permute-done.10.refs_3_
  37.0 1.5 %collective-permute-start.8 = (f32[32,384]{1,0:T(8,128)S(1)}, f32[32,384]{1,0:T(8,128)S(1)}, u32[]{:S(2)}, u32[]{:S(2)}) collective-permute-start(f32[32,384]{1,0:T(8,128)S(1)} %get-tuple-element.39), channel_id=1, source_target_pairs={{0,2},{2,0},{4,6},{6,4},{8,10},{10,8},{12,14},{14,12},{1,3},{3,1},... | collective-permute-start | bytes 147464 | tf_op jit(solution)/shard_map/ppermute | solution.py:380
  38.5 0.0 collective-permute-done.11.refs_4_
  38.5 0.0 collective-permute-start.9
  38.5 1.1 %shard_map.131.refs_0_ = f32[32,384]{1,0:T(8,128)S(1)} custom-call(f32[4096,128]{1,0:T(8,128)S(1)} %get-tuple-element.38.grid_ref, s32[3072]{0:T(1024)S(1)} %bitcast.35, s32[24,128]{1,0:T(8,128)S(1)} %get-tuple-element.37.refs_6_.refs_5_.cols_ref), custom_call_target="tpu_custom_call" | custom-call | flops 1073741824 | bytes 1048576 | tf_op jit(solution)/shard_map/pallas_call | solution.py:320
  39.6 0.0 collective-permute-done.12.refs_5_
  39.7 0.0 collective-permute-done.13.refs_6_
  39.7 2.3 %collective-permute-done.14.refs_7_ = f32[32,384]{1,0:T(8,128)S(1)} collective-permute-done((f32[32,384]{1,0:T(8,128)S(1)}, f32[32,384]{1,0:T(8,128)S(1)}, u32[]{:S(2)}, u32[]{:S(2)}) %collective-permute-start.14) | collective-permute-done | bytes 49184 | tf_op jit(solution)/shard_map/ppermute | solution.py:380
  42.0 0.7 %collective-permute-done.9.refs_2_ = f32[32,384]{1,0:T(8,128)S(1)} collective-permute-done((f32[32,384]{1,0:T(8,128)S(1)}, f32[32,384]{1,0:T(8,128)S(1)}, u32[]{:S(2)}, u32[]{:S(2)}) %collective-permute-start.9) | collective-permute-done | bytes 49184 | tf_op jit(solution)/shard_map/ppermute | solution.py:380
  42.6 0.6 %shard_map.132 = (f32[2,96,128]{2,1,0:T(8,128)S(1)}, f32[2,96,128]{2,1,0:T(8,128)S(1)}) custom-call(f32[32,384]{1,0:T(8,128)S(1)} %shard_map.131.refs_0_, f32[32,384]{1,0:T(8,128)S(1)} %collective-permute-done.8.refs_1_, f32[32,384]{1,0:T(8,128)S(1)} %collective-permute-done.9.refs_2_, f32[32,384]{1,0:T(8,128)S(1)} %collective-permute-done.10.refs_3_, ...), custom_call_target="tpu_custom_call" | custom-call | flops 1073741824 | bytes 1048576 | tf_op jit(solution)/shard_map/pallas_call | solution.py:320
  43.2 0.1 collective-permute-start.15
  43.3 0.1 copy.21
  43.4 1.2 %collective-permute-done.15 = f32[2,96,128]{2,1,0:T(8,128)S(1)} collective-permute-done((f32[2,96,128]{2,1,0:T(8,128)S(1)}, f32[2,96,128]{2,1,0:T(8,128)S(1)}, u32[]{:S(2)}, u32[]{:S(2)}) %collective-permute-start.15) | collective-permute-done | bytes 98336 | tf_op jit(solution)/shard_map/ppermute | solution.py:432
  44.6 0.1 copy.20
  44.6 0.8 %broadcast_select_fusion = f32[2,2,12288]{2,1,0:T(2,128)} fusion(pred[2]{0:T(512)(128)(4,1)S(1)} %iota_compare_fusion, f32[2,12288]{1,0:T(2,128)S(1)} %bitcast.37, f32[2,12288]{1,0:T(2,128)S(1)} %bitcast.36), kind=kLoop, calls=%fused_computation | loop fusion | flops 49152 | bytes 393218 | tf_op jit(solution)/shard_map/jit(_where)/select_n | solution.py:436
  (16 shorter events, 0.0 us)
Async XLA Ops:
  0.0 2.0 %copy-start.2 = (f32[2,2,12288]{2,1,0:T(2,128)S(1)}, f32[2,2,12288]{2,1,0:T(2,128)}, u32[]{:S(2)}) copy-start(f32[2,2,12288]{2,1,0:T(2,128)} %param.13) | copy-start | bytes 589828
  0.0 2.0 %collective-permute-start = (f32[2,192,128]{2,1,0:T(8,128)}, f32[2,192,128]{2,1,0:T(8,128)S(1)}, u32[]{:S(2)}, u32[]{:S(2)}) collective-permute-start(f32[2,192,128]{2,1,0:T(8,128)} %bitcast.29), channel_id=1, source_target_pairs={{0,1},{1,0},{2,3},{3,2},{4,5},{5,4},{6,7},{7,6},{8,9},{9,8},{10,11... | collective-permute-start | bytes 589832 | tf_op jit(solution)/shard_map/ppermute | solution.py:352
  0.5 0.9 %copy-start.3 = (s32[384,64]{0,1:T(8,128)S(1)}, s32[384,64]{0,1:T(8,128)}, u32[]{:S(2)}) copy-start(s32[384,64]{0,1:T(8,128)} %param.15) | copy-start | bytes 294916
  1.4 0.7 %copy-start.4 = (s32[3072]{0:T(1024)S(1)}, s32[3072]{0:T(1024)}, u32[]{:S(2)}) copy-start(s32[3072]{0:T(1024)} %param.14) | copy-start | bytes 36868
  1.4 0.9 %copy-start.5 = (bf16[256,256]{1,0:T(8,128)(2,1)S(1)}, bf16[256,256]{1,0:T(8,128)(2,1)}, u32[]{:S(2)}) copy-start(bf16[256,256]{1,0:T(8,128)(2,1)} %constant.20.clone.high_ref.refs_9_) | copy-start | bytes 393220
  1.4 1.0 %copy-start.6 = (bf16[256,256]{1,0:T(8,128)(2,1)S(1)}, bf16[256,256]{1,0:T(8,128)(2,1)}, u32[]{:S(2)}) copy-start(bf16[256,256]{1,0:T(8,128)(2,1)} %constant.21.clone.low_ref.refs_10_) | copy-start | bytes 393220
  3.2 16.1 %copy-start = (f32[16,16384]{1,0:T(8,128)S(1)}, f32[16,16384]{1,0:T(8,128)}, u32[]{:S(2)}) copy-start(f32[16,16384]{1,0:T(8,128)} %param.16) | copy-start | bytes 3145732
  3.2 16.1 %copy-start.1 = (f32[16,16384]{1,0:T(8,128)S(1)}, f32[16,16384]{1,0:T(8,128)}, u32[]{:S(2)}) copy-start(f32[16,16384]{1,0:T(8,128)} %param.17) | copy-start | bytes 3145732
  3.2 16.1 %copy-start.7 = (bf16[256,256]{1,0:T(8,128)(2,1)S(1)}, bf16[256,256]{1,0:T(8,128)(2,1)}, u32[]{:S(2)}) copy-start(bf16[256,256]{1,0:T(8,128)(2,1)} %constant.16.clone.refs_8_) | copy-start | bytes 393220
  3.2 16.1 %copy-start.8 = (bf16[256,256]{1,0:T(8,128)(2,1)S(1)}, bf16[256,256]{1,0:T(8,128)(2,1)}, u32[]{:S(2)}) copy-start(bf16[256,256]{1,0:T(8,128)(2,1)} %constant.17.clone.refs_9_) | copy-start | bytes 393220
  3.2 16.1 %copy-start.9 = (bf16[256,256]{1,0:T(8,128)(2,1)S(1)}, bf16[256,256]{1,0:T(8,128)(2,1)}, u32[]{:S(2)}) copy-start(bf16[256,256]{1,0:T(8,128)(2,1)} %constant.18.clone.refs_10_) | copy-start | bytes 393220
  3.2 16.1 %copy-start.10 = (bf16[256,256]{1,0:T(8,128)(2,1)S(1)}, bf16[256,256]{1,0:T(8,128)(2,1)}, u32[]{:S(2)}) copy-start(bf16[256,256]{1,0:T(8,128)(2,1)} %constant.19.clone.refs_11_) | copy-start | bytes 393220
  3.2 10.0 %collective-permute-start.4 = (f32[32,384]{1,0:T(8,128)S(1)}, f32[32,384]{1,0:T(8,128)S(1)}, u32[]{:S(2)}, u32[]{:S(2)}) collective-permute-start(f32[32,384]{1,0:T(8,128)S(1)} %get-tuple-element.32), channel_id=1, source_target_pairs={{0,12},{2,14},{4,8},{6,10},{8,4},{10,6},{12,0},{14,2},{1,13},{3,15... | collective-permute-start | bytes 147464 | tf_op jit(solution)/shard_map/ppermute | solution.py:380
  7.9 6.3 %collective-permute-start.5 = (f32[32,384]{1,0:T(8,128)S(1)}, f32[32,384]{1,0:T(8,128)S(1)}, u32[]{:S(2)}, u32[]{:S(2)}) collective-permute-start(f32[32,384]{1,0:T(8,128)S(1)} %get-tuple-element.33), channel_id=1, source_target_pairs={{0,8},{2,10},{4,12},{6,14},{8,0},{10,2},{12,4},{14,6},{1,9},{3,11}... | collective-permute-start | bytes 147464 | tf_op jit(solution)/shard_map/ppermute | solution.py:380
  7.9 8.1 %collective-permute-start.6 = (f32[32,384]{1,0:T(8,128)S(1)}, f32[32,384]{1,0:T(8,128)S(1)}, u32[]{:S(2)}, u32[]{:S(2)}) collective-permute-start(f32[32,384]{1,0:T(8,128)S(1)} %get-tuple-element.34), channel_id=1, source_target_pairs={{0,14},{2,12},{4,10},{6,8},{8,6},{10,4},{12,2},{14,0},{1,15},{3,13... | collective-permute-start | bytes 147464 | tf_op jit(solution)/shard_map/ppermute | solution.py:380
  10.8 5.2 %collective-permute-start.7 = (f32[32,384]{1,0:T(8,128)S(1)}, f32[32,384]{1,0:T(8,128)S(1)}, u32[]{:S(2)}, u32[]{:S(2)}) collective-permute-start(f32[32,384]{1,0:T(8,128)S(1)} %get-tuple-element.35), channel_id=1, source_target_pairs={{0,4},{2,6},{4,0},{6,2},{8,12},{10,14},{12,8},{14,10},{1,5},{3,7},... | collective-permute-start | bytes 147464 | tf_op jit(solution)/shard_map/ppermute | solution.py:380
  12.4 6.5 %collective-permute-start.1 = (f32[32,384]{1,0:T(8,128)S(1)}, f32[32,384]{1,0:T(8,128)S(1)}, u32[]{:S(2)}, u32[]{:S(2)}) collective-permute-start(f32[32,384]{1,0:T(8,128)S(1)} %get-tuple-element.28), channel_id=1, source_target_pairs={{0,10},{2,8},{4,14},{6,12},{8,2},{10,0},{12,6},{14,4},{1,11},{3,9}... | collective-permute-start | bytes 147464 | tf_op jit(solution)/shard_map/ppermute | solution.py:380
  13.2 5.6 %collective-permute-start.2 = (f32[32,384]{1,0:T(8,128)S(1)}, f32[32,384]{1,0:T(8,128)S(1)}, u32[]{:S(2)}, u32[]{:S(2)}) collective-permute-start(f32[32,384]{1,0:T(8,128)S(1)} %get-tuple-element.29), channel_id=1, source_target_pairs={{0,6},{2,4},{4,2},{6,0},{8,14},{10,12},{12,10},{14,8},{1,7},{3,5},... | collective-permute-start | bytes 147464 | tf_op jit(solution)/shard_map/ppermute | solution.py:380
  14.2 5.1 %collective-permute-start.3 = (f32[32,384]{1,0:T(8,128)S(1)}, f32[32,384]{1,0:T(8,128)S(1)}, u32[]{:S(2)}, u32[]{:S(2)}) collective-permute-start(f32[32,384]{1,0:T(8,128)S(1)} %get-tuple-element.30), channel_id=1, source_target_pairs={{0,2},{2,0},{4,6},{6,4},{8,10},{10,8},{12,14},{14,12},{1,3},{3,1},... | collective-permute-start | bytes 147464 | tf_op jit(solution)/shard_map/ppermute | solution.py:380
  28.3 8.7 %collective-permute-start.10 = (f32[32,384]{1,0:T(8,128)S(1)}, f32[32,384]{1,0:T(8,128)S(1)}, u32[]{:S(2)}, u32[]{:S(2)}) collective-permute-start(f32[32,384]{1,0:T(8,128)S(1)} %get-tuple-element.41), channel_id=1, source_target_pairs={{0,6},{2,4},{4,2},{6,0},{8,14},{10,12},{12,10},{14,8},{1,7},{3,5},... | collective-permute-start | bytes 147464 | tf_op jit(solution)/shard_map/ppermute | solution.py:380
  29.4 9.2 %collective-permute-start.11 = (f32[32,384]{1,0:T(8,128)S(1)}, f32[32,384]{1,0:T(8,128)S(1)}, u32[]{:S(2)}, u32[]{:S(2)}) collective-permute-start(f32[32,384]{1,0:T(8,128)S(1)} %get-tuple-element.42), channel_id=1, source_target_pairs={{0,8},{2,10},{4,12},{6,14},{8,0},{10,2},{12,4},{14,6},{1,9},{3,11}... | collective-permute-start | bytes 147464 | tf_op jit(solution)/shard_map/ppermute | solution.py:380
  31.4 8.3 %collective-permute-start.12 = (f32[32,384]{1,0:T(8,128)S(1)}, f32[32,384]{1,0:T(8,128)S(1)}, u32[]{:S(2)}, u32[]{:S(2)}) collective-permute-start(f32[32,384]{1,0:T(8,128)S(1)} %get-tuple-element.43), channel_id=1, source_target_pairs={{0,10},{2,8},{4,14},{6,12},{8,2},{10,0},{12,6},{14,4},{1,11},{3,9}... | collective-permute-start | bytes 147464 | tf_op jit(solution)/shard_map/ppermute | solution.py:380
  33.2 6.4 %collective-permute-start.13 = (f32[32,384]{1,0:T(8,128)S(1)}, f32[32,384]{1,0:T(8,128)S(1)}, u32[]{:S(2)}, u32[]{:S(2)}) collective-permute-start(f32[32,384]{1,0:T(8,128)S(1)} %get-tuple-element.44), channel_id=1, source_target_pairs={{0,12},{2,14},{4,8},{6,10},{8,4},{10,6},{12,0},{14,2},{1,13},{3,15... | collective-permute-start | bytes 147464 | tf_op jit(solution)/shard_map/ppermute | solution.py:380
  35.2 6.8 %collective-permute-start.14 = (f32[32,384]{1,0:T(8,128)S(1)}, f32[32,384]{1,0:T(8,128)S(1)}, u32[]{:S(2)}, u32[]{:S(2)}) collective-permute-start(f32[32,384]{1,0:T(8,128)S(1)} %get-tuple-element.45), channel_id=1, source_target_pairs={{0,14},{2,12},{4,10},{6,8},{8,6},{10,4},{12,2},{14,0},{1,15},{3,13... | collective-permute-start | bytes 147464 | tf_op jit(solution)/shard_map/ppermute | solution.py:380
  37.0 4.9 %collective-permute-start.8 = (f32[32,384]{1,0:T(8,128)S(1)}, f32[32,384]{1,0:T(8,128)S(1)}, u32[]{:S(2)}, u32[]{:S(2)}) collective-permute-start(f32[32,384]{1,0:T(8,128)S(1)} %get-tuple-element.39), channel_id=1, source_target_pairs={{0,2},{2,0},{4,6},{6,4},{8,10},{10,8},{12,14},{14,12},{1,3},{3,1},... | collective-permute-start | bytes 147464 | tf_op jit(solution)/shard_map/ppermute | solution.py:380
  38.5 4.1 %collective-permute-start.9 = (f32[32,384]{1,0:T(8,128)S(1)}, f32[32,384]{1,0:T(8,128)S(1)}, u32[]{:S(2)}, u32[]{:S(2)}) collective-permute-start(f32[32,384]{1,0:T(8,128)S(1)} %get-tuple-element.40), channel_id=1, source_target_pairs={{0,4},{2,6},{4,0},{6,2},{8,12},{10,14},{12,8},{14,10},{1,5},{3,7},... | collective-permute-start | bytes 147464 | tf_op jit(solution)/shard_map/ppermute | solution.py:380
  43.2 1.4 %collective-permute-start.15 = (f32[2,96,128]{2,1,0:T(8,128)S(1)}, f32[2,96,128]{2,1,0:T(8,128)S(1)}, u32[]{:S(2)}, u32[]{:S(2)}) collective-permute-start(f32[2,96,128]{2,1,0:T(8,128)S(1)} %get-tuple-element.48), channel_id=1, source_target_pairs={{0,1},{1,0},{2,3},{3,2},{4,5},{5,4},{6,7},{7,6},{8,9},{9,8},{10,11... | collective-permute-start | bytes 294920 | tf_op jit(solution)/shard_map/ppermute | solution.py:432
